TPU v7x, 128 devices: a whole 4x4x4 slice. The times are simulated.
128 devices in a mesh: col: 16 (over x, y), cuts: 8 (over z, core).
Axes of the slice: x: 4, y: 4, z: 4, core: 2. Of those that a mesh axis runs over, the one named last changes fastest.
Arguments:
- layout: int32 [16, 16], P(None, 'col'), may hold values from 0 to 15
- assign: int32 [32, 16], P('cuts', 'col'), may hold values from 0 to 3
- edge: bfloat16 [16, 64, 128], replicated, may hold values from -3 to 3
- gate_left: bfloat16 [16, 16, 64, 128], P('col'), may hold values from -1.5 to 1.5
- gate_right: bfloat16 [16, 16, 64, 128], P('col'), may hold values from -1.5 to 1.5
- phase_angle: float32 [4, 64], replicated, may hold values from -3.140625 to 3.140625
- close: float32 [16, 64, 128], replicated, may hold values from -6 to 6
Outputs:
- slice_amplitude: float32 [32, 2], P('cuts')
- slice_log: float32 [32], P('cuts')
- total_amp: float32 [2], replicated
- top_log: float32 [], replicated
All inputs are finite; a program needn't handle non-finite values. Where the computation divides by a largest or mean magnitude, that divisor is 1e-20 or more.
Results may differ from a plain program's by a relative error of at most 0.0003.
Values sent between devices are 32-bit elements; how exact they have to be, the bound alone decides.
No kernel may reach another device: no remote copies, remote signals or barrier semaphores. Data moves between devices by JAX's collectives and lax.ppermute only.
A program may use at most 64 MiB of HBM per device.

v0:
```python
import math
import jax
import jax.numpy as jnp
from jax import lax
from jax.sharding import Mesh
from jax.sharding import PartitionSpec as P

BLK = 1
COL = ("col_0", "col_1")


def from_behind(value, axis, by):
    length = lax.axis_size(axis)
    pairs = [(i, i + by) for i in range(length) if 0 <= i + by < length]
    return lax.ppermute(value, axis, pairs)


def over_axes(value, axes):
    for axis in axes:
        value = lax.psum(value, axis)
    return value


def from_everyone(value, axis):
    length = lax.axis_size(axis)
    return lax.all_to_all(
        jnp.broadcast_to(value[None], (length, *value.shape)), axis, 0, 0, tiled=True
    )


def of_everyone(value, axis):
    return from_everyone(value, axis).max(axis=0)


def taken_together(value, axis):
    everything = from_everyone(value, axis)
    return jnp.sum(everything, axis=0)


def one_hot(values, count, dtype):
    return (values[..., None] == jnp.arange(count, dtype=jnp.int32)).astype(dtype)


def sweep_column(board, left_sel, right_sel, cosine, sine):
    width = board.shape[-2]
    below = jnp.concatenate([board[:, 1:], jnp.zeros_like(board[:, :1])], axis=1)
    mixed = board + 0.5 * below
    left_four = left_sel.reshape(left_sel.shape[0], width, 2, width)
    stacked = jnp.einsum("rpka,srab->srkpb", left_four, mixed, precision=lax.Precision.HIGHEST)
    former = stacked[:, :, 0]
    latter = stacked[:, :, 1]
    real_part = former[..., :width] - latter[..., width:]
    imag_part = former[..., width:] + latter[..., :width]
    from_real = jnp.einsum("srab,rbq->sraq", real_part, right_sel, precision=lax.Precision.HIGHEST)
    from_imag = jnp.einsum("srab,rbq->sraq", imag_part, right_sel, precision=lax.Precision.HIGHEST)
    out_real = from_real[..., :width] - from_imag[..., width:]
    out_imag = from_real[..., width:] + from_imag[..., :width]
    cos_rows = cosine[:, None, None, :]
    sin_rows = sine[:, None, None, :]
    turned_real = out_real * cos_rows - out_imag * sin_rows
    turned_imag = out_real * sin_rows + out_imag * cos_rows
    peaks = jnp.maximum(
        jnp.max(jnp.abs(turned_real), axis=(1, 2, 3)), jnp.max(jnp.abs(turned_imag), axis=(1, 2, 3))
    )
    peaks = jnp.maximum(peaks, 1.0)
    board = jnp.concatenate([turned_real, turned_imag], -1) / peaks[:, None, None, None]
    return (board, jnp.log(peaks))


def amplitude(board, close):
    width = close.shape[-1] // 2
    b_real = board[..., :width]
    b_imag = board[..., width:]
    c_real = close[..., :width]
    c_imag = close[..., width:]
    factor = 1.0 / math.sqrt(close.shape[0] * width * width)
    amp_real = jnp.sum(b_real * c_real - b_imag * c_imag, axis=(1, 2, 3)) * factor
    amp_imag = jnp.sum(b_real * c_imag + b_imag * c_real, axis=(1, 2, 3)) * factor
    return jnp.stack([amp_real, amp_imag], -1)


def body(layout, assign, edge, gate_left, gate_right, phase_angle, close):
    sections = lax.axis_size(COL)
    place = lax.axis_index(COL)
    kinds = gate_left.shape[1]
    values = phase_angle.shape[0]
    per_device = assign.shape[0]
    group = BLK
    groups = per_device // group
    row_hot = one_hot(layout.T, kinds, jnp.bfloat16)
    left_all = jnp.einsum("crg,cgpq->crpq", row_hot, gate_left, preferred_element_type=jnp.float32)
    right_all = jnp.einsum(
        "crg,cgpq->crpq", row_hot, gate_right, preferred_element_type=jnp.float32
    )
    cos_table = jnp.cos(phase_angle)
    sin_table = jnp.sin(phase_angle)
    start_board = edge.astype(jnp.float32)[None]

    def run_columns(board, assign_group):
        value_hot = one_hot(assign_group, values, jnp.float32)
        cos_sel = jnp.einsum("scq,qb->scb", value_hot, cos_table, precision=lax.Precision.HIGHEST)
        sin_sel = jnp.einsum("scq,qb->scb", value_hot, sin_table, precision=lax.Precision.HIGHEST)
        board, scales = sweep_column(board, left_all[0], right_all[0], cos_sel[:, 0], sin_sel[:, 0])
        return (board, scales)

    def section(step, carry):
        held_board, amps, logs = carry
        index = step - place
        valid = jnp.logical_and(index >= 0, index < groups)
        safe = jnp.clip(index, 0, groups - 1)
        first = place == 0
        board = jnp.where(first, start_board, held_board)
        assign_group = lax.dynamic_slice_in_dim(assign, safe * group, group, 0)
        board, scales = lax.cond(
            valid,
            lambda: run_columns(board, assign_group),
            lambda: (board, jnp.zeros((group,), jnp.float32)),
        )
        keep = jnp.logical_and(valid, place == sections - 1)
        amps = jnp.where(
            keep,
            lax.dynamic_update_slice_in_dim(amps, amplitude(board, close), safe * group, 0),
            amps,
        )
        logs = jnp.where(
            valid, lax.dynamic_update_slice_in_dim(logs, scales, safe * group, 0), logs
        )
        held_board = from_behind(board, COL, 1)
        return (held_board, amps, logs)

    initial = (
        start_board,
        jnp.zeros((per_device, 2), jnp.float32),
        jnp.zeros((per_device,), jnp.float32),
    )
    unused_board, amps, logs = lax.fori_loop(0, sections + groups - 1, section, initial)
    amps, logs = (over_axes(amps, COL), over_axes(logs, COL))
    local_top = jnp.max(logs)
    top_log = of_everyone(local_top, "cuts")
    partial_sum = jnp.sum(amps * jnp.exp(logs - top_log)[:, None], axis=0)
    total_amp = taken_together(partial_sum, "cuts")
    return (amps, logs, total_amp, top_log)


def solution(mesh):
    split = Mesh(mesh.devices.reshape(4, 4, mesh.shape["cuts"]), ("col_0", "col_1", "cuts"))
    placed = (
        P(None, COL),
        P("cuts", COL),
        P(),
        P(COL, None, None, None),
        P(COL, None, None, None),
        P(),
        P(),
    )
    return jax.shard_map(
        body,
        mesh=split,
        in_specs=placed,
        out_specs=(P("cuts", None), P("cuts"), P(), P()),
        check_vma=False,
    )
```

profile of v0, /device:TPU:1, one launch (start us, length us, event | category | flops | bytes accessed | tf_op | source)
XLA Modules:
  0.0 458.8 jit_solution(4643942819988756618)
XLA Ops:
  6.2 341.0 %while.18 = (s32[]{:T(128)}, f32[1,16,64,128]{3,2,1,0:T(8,128)S(1)}, f32[4,2]{0,1:T(2,128)S(1)}, f32[4]{0:T(128)S(1)}, s32[]{:T(128)}, /*index=5*/pred[]{:T(512)...) while((s32[]{:T(128)}, ...), condition=%wide.region_7.8_spmd, body=%wide.region_0.7_spmd.sunk | while | flops 404756480 | bytes 22449744 | solution.py:136
  7.0 8.9 %conditional.2 = (f32[1,16,64,128]{3,2,1,0:T(8,128)S(1)}, f32[1]{0:T(128)}) conditional(s32[]{:T(128)} %convert_element_type.12, f32[1,16,64,128]{3,2,1,0:T(8,128)S(1)} %broadcast_select_fusion.2, (f32[1,16,64,128]{3,2,1,0:T(8,128)S(1)}, f32[1,16,64,128]{3,2,1,0:T(8,128)}, f32[1,16,64,128]{3,2,1,0:T(8,128)S(1)}, s32[4,1]{0,1:T(1,128)S(1)}, s32[]{:T(128)}, ...), branch_computations={%region_1.1_spmd, %region_2.4_spmd} | conditional | flops 404101120 | bytes 13536336 | solution.py:114
  19.8 7.7 %collective-permute-done = f32[1,16,64,128]{3,2,1,0:T(8,128)S(1)} collective-permute-done((f32[1,16,64,128]{3,2,1,0:T(8,128)S(1)}, f32[1,16,64,128]{3,2,1,0:T(8,128)S(1)}, u32[]{:S(2)}, u32[]{:S(2)}) %collective-permute-start) | collective-permute-done | bytes 524320 | tf_op jit(solution)/shard_map/while/body/eval_jaxpr/ppermute | solution.py:15
  28.3 8.9 %conditional.2 = (f32[1,16,64,128]{3,2,1,0:T(8,128)S(1)}, f32[1]{0:T(128)}) conditional(s32[]{:T(128)} %convert_element_type.12, f32[1,16,64,128]{3,2,1,0:T(8,128)S(1)} %broadcast_select_fusion.2, (f32[1,16,64,128]{3,2,1,0:T(8,128)S(1)}, f32[1,16,64,128]{3,2,1,0:T(8,128)}, f32[1,16,64,128]{3,2,1,0:T(8,128)S(1)}, s32[4,1]{0,1:T(1,128)S(1)}, s32[]{:T(128)}, ...), branch_computations={%region_1.1_spmd, %region_2.4_spmd} | conditional | flops 404101120 | bytes 13536336 | solution.py:114
  43.9 6.7 %collective-permute-done = f32[1,16,64,128]{3,2,1,0:T(8,128)S(1)} collective-permute-done((f32[1,16,64,128]{3,2,1,0:T(8,128)S(1)}, f32[1,16,64,128]{3,2,1,0:T(8,128)S(1)}, u32[]{:S(2)}, u32[]{:S(2)}) %collective-permute-start) | collective-permute-done | bytes 524320 | tf_op jit(solution)/shard_map/while/body/eval_jaxpr/ppermute | solution.py:15
  51.4 8.9 %conditional.2 = (f32[1,16,64,128]{3,2,1,0:T(8,128)S(1)}, f32[1]{0:T(128)}) conditional(s32[]{:T(128)} %convert_element_type.12, f32[1,16,64,128]{3,2,1,0:T(8,128)S(1)} %broadcast_select_fusion.2, (f32[1,16,64,128]{3,2,1,0:T(8,128)S(1)}, f32[1,16,64,128]{3,2,1,0:T(8,128)}, f32[1,16,64,128]{3,2,1,0:T(8,128)S(1)}, s32[4,1]{0,1:T(1,128)S(1)}, s32[]{:T(128)}, ...), branch_computations={%region_1.1_spmd, %region_2.4_spmd} | conditional | flops 404101120 | bytes 13536336 | solution.py:114
  73.8 8.9 %conditional.2 = (f32[1,16,64,128]{3,2,1,0:T(8,128)S(1)}, f32[1]{0:T(128)}) conditional(s32[]{:T(128)} %convert_element_type.12, f32[1,16,64,128]{3,2,1,0:T(8,128)S(1)} %broadcast_select_fusion.2, (f32[1,16,64,128]{3,2,1,0:T(8,128)S(1)}, f32[1,16,64,128]{3,2,1,0:T(8,128)}, f32[1,16,64,128]{3,2,1,0:T(8,128)S(1)}, s32[4,1]{0,1:T(1,128)S(1)}, s32[]{:T(128)}, ...), branch_computations={%region_1.1_spmd, %region_2.4_spmd} | conditional | flops 404101120 | bytes 13536336 | solution.py:114
  95.2 13.1 %collective-permute-start = (f32[1,16,64,128]{3,2,1,0:T(8,128)S(1)}, f32[1,16,64,128]{3,2,1,0:T(8,128)S(1)}, u32[]{:S(2)}, u32[]{:S(2)}) collective-permute-start(f32[1,16,64,128]{3,2,1,0:T(8,128)S(1)} %get-tuple-element.477), channel_id=1, source_target_pairs={{0,8},{8,16},{16,24},{24,32},{32,40},{40,48},{48,56},{56,64},{64,7... | collective-permute-start | bytes 1572872 | tf_op jit(solution)/shard_map/while/body/eval_jaxpr/ppermute | solution.py:15
  126.8 12.0 %collective-permute-start = (f32[1,16,64,128]{3,2,1,0:T(8,128)S(1)}, f32[1,16,64,128]{3,2,1,0:T(8,128)S(1)}, u32[]{:S(2)}, u32[]{:S(2)}) collective-permute-start(f32[1,16,64,128]{3,2,1,0:T(8,128)S(1)} %get-tuple-element.477), channel_id=1, source_target_pairs={{0,8},{8,16},{16,24},{24,32},{32,40},{40,48},{48,56},{56,64},{64,7... | collective-permute-start | bytes 1572872 | tf_op jit(solution)/shard_map/while/body/eval_jaxpr/ppermute | solution.py:15
  158.0 13.7 %collective-permute-start = (f32[1,16,64,128]{3,2,1,0:T(8,128)S(1)}, f32[1,16,64,128]{3,2,1,0:T(8,128)S(1)}, u32[]{:S(2)}, u32[]{:S(2)}) collective-permute-start(f32[1,16,64,128]{3,2,1,0:T(8,128)S(1)} %get-tuple-element.477), channel_id=1, source_target_pairs={{0,8},{8,16},{16,24},{24,32},{32,40},{40,48},{48,56},{56,64},{64,7... | collective-permute-start | bytes 1572872 | tf_op jit(solution)/shard_map/while/body/eval_jaxpr/ppermute | solution.py:15
  191.8 14.8 %collective-permute-start = (f32[1,16,64,128]{3,2,1,0:T(8,128)S(1)}, f32[1,16,64,128]{3,2,1,0:T(8,128)S(1)}, u32[]{:S(2)}, u32[]{:S(2)}) collective-permute-start(f32[1,16,64,128]{3,2,1,0:T(8,128)S(1)} %get-tuple-element.477), channel_id=1, source_target_pairs={{0,8},{8,16},{16,24},{24,32},{32,40},{40,48},{48,56},{56,64},{64,7... | collective-permute-start | bytes 1572872 | tf_op jit(solution)/shard_map/while/body/eval_jaxpr/ppermute | solution.py:15
  213.5 8.1 %collective-permute-start = (f32[1,16,64,128]{3,2,1,0:T(8,128)S(1)}, f32[1,16,64,128]{3,2,1,0:T(8,128)S(1)}, u32[]{:S(2)}, u32[]{:S(2)}) collective-permute-start(f32[1,16,64,128]{3,2,1,0:T(8,128)S(1)} %get-tuple-element.477), channel_id=1, source_target_pairs={{0,8},{8,16},{16,24},{24,32},{32,40},{40,48},{48,56},{56,64},{64,7... | collective-permute-start | bytes 1572872 | tf_op jit(solution)/shard_map/while/body/eval_jaxpr/ppermute | solution.py:15
  237.7 6.6 %collective-permute-done = f32[1,16,64,128]{3,2,1,0:T(8,128)S(1)} collective-permute-done((f32[1,16,64,128]{3,2,1,0:T(8,128)S(1)}, f32[1,16,64,128]{3,2,1,0:T(8,128)S(1)}, u32[]{:S(2)}, u32[]{:S(2)}) %collective-permute-start) | collective-permute-done | bytes 524320 | tf_op jit(solution)/shard_map/while/body/eval_jaxpr/ppermute | solution.py:15
  245.1 17.0 %collective-permute-start = (f32[1,16,64,128]{3,2,1,0:T(8,128)S(1)}, f32[1,16,64,128]{3,2,1,0:T(8,128)S(1)}, u32[]{:S(2)}, u32[]{:S(2)}) collective-permute-start(f32[1,16,64,128]{3,2,1,0:T(8,128)S(1)} %get-tuple-element.477), channel_id=1, source_target_pairs={{0,8},{8,16},{16,24},{24,32},{32,40},{40,48},{48,56},{56,64},{64,7... | collective-permute-start | bytes 1572872 | tf_op jit(solution)/shard_map/while/body/eval_jaxpr/ppermute | solution.py:15
  264.6 8.6 %collective-permute-done = f32[1,16,64,128]{3,2,1,0:T(8,128)S(1)} collective-permute-done((f32[1,16,64,128]{3,2,1,0:T(8,128)S(1)}, f32[1,16,64,128]{3,2,1,0:T(8,128)S(1)}, u32[]{:S(2)}, u32[]{:S(2)}) %collective-permute-start) | collective-permute-done | bytes 524320 | tf_op jit(solution)/shard_map/while/body/eval_jaxpr/ppermute | solution.py:15
  282.8 7.4 %collective-permute-done = f32[1,16,64,128]{3,2,1,0:T(8,128)S(1)} collective-permute-done((f32[1,16,64,128]{3,2,1,0:T(8,128)S(1)}, f32[1,16,64,128]{3,2,1,0:T(8,128)S(1)}, u32[]{:S(2)}, u32[]{:S(2)}) %collective-permute-start) | collective-permute-done | bytes 524320 | tf_op jit(solution)/shard_map/while/body/eval_jaxpr/ppermute | solution.py:15
  298.6 6.3 %collective-permute-done = f32[1,16,64,128]{3,2,1,0:T(8,128)S(1)} collective-permute-done((f32[1,16,64,128]{3,2,1,0:T(8,128)S(1)}, f32[1,16,64,128]{3,2,1,0:T(8,128)S(1)}, u32[]{:S(2)}, u32[]{:S(2)}) %collective-permute-start) | collective-permute-done | bytes 524320 | tf_op jit(solution)/shard_map/while/body/eval_jaxpr/ppermute | solution.py:15
  305.7 6.2 %collective-permute-start = (f32[1,16,64,128]{3,2,1,0:T(8,128)S(1)}, f32[1,16,64,128]{3,2,1,0:T(8,128)S(1)}, u32[]{:S(2)}, u32[]{:S(2)}) collective-permute-start(f32[1,16,64,128]{3,2,1,0:T(8,128)S(1)} %get-tuple-element.477), channel_id=1, source_target_pairs={{0,8},{8,16},{16,24},{24,32},{32,40},{40,48},{48,56},{56,64},{64,7... | collective-permute-start | bytes 1572872 | tf_op jit(solution)/shard_map/while/body/eval_jaxpr/ppermute | solution.py:15
  320.7 6.2 %collective-permute-start = (f32[1,16,64,128]{3,2,1,0:T(8,128)S(1)}, f32[1,16,64,128]{3,2,1,0:T(8,128)S(1)}, u32[]{:S(2)}, u32[]{:S(2)}) collective-permute-start(f32[1,16,64,128]{3,2,1,0:T(8,128)S(1)} %get-tuple-element.477), channel_id=1, source_target_pairs={{0,8},{8,16},{16,24},{24,32},{32,40},{40,48},{48,56},{56,64},{64,7... | collective-permute-start | bytes 1572872 | tf_op jit(solution)/shard_map/while/body/eval_jaxpr/ppermute | solution.py:15
  334.9 6.2 %collective-permute-start = (f32[1,16,64,128]{3,2,1,0:T(8,128)S(1)}, f32[1,16,64,128]{3,2,1,0:T(8,128)S(1)}, u32[]{:S(2)}, u32[]{:S(2)}) collective-permute-start(f32[1,16,64,128]{3,2,1,0:T(8,128)S(1)} %get-tuple-element.477), channel_id=1, source_target_pairs={{0,8},{8,16},{16,24},{24,32},{32,40},{40,48},{48,56},{56,64},{64,7... | collective-permute-start | bytes 1572872 | tf_op jit(solution)/shard_map/while/body/eval_jaxpr/ppermute | solution.py:15
  347.2 53.0 %all-reduce.2 = (f32[4,2]{0,1:T(2,128)S(1)}, f32[4]{0:T(128)S(1)}) all-reduce(f32[4,2]{0,1:T(2,128)S(1)} %get-tuple-element.300, f32[4]{0:T(128)S(1)} %get-tuple-element.301), channel_id=1, replica_groups=mesh['col_0'=4,'col_1'=4,'cuts'=8] {'col_0'}, use_global_device_ids=true, to_apply=%region_8.9 | all-reduce | flops 12 | bytes 96 | tf_op jit(solution)/shard_map/psum | solution.py:20
  400.2 12.3 %all-reduce.1 = (f32[4,2]{0,1:T(2,128)S(1)}, f32[4]{0:T(128)S(1)}) all-reduce(f32[4,2]{0,1:T(2,128)S(1)} %get-tuple-element.376, f32[4]{0:T(128)S(1)} %get-tuple-element.377), channel_id=1, replica_groups=mesh['col_0'=4,'col_1'=4,'cuts'=8] {'col_1'}, use_global_device_ids=true, to_apply=%region_9.10 | all-reduce | flops 12 | bytes 96 | tf_op jit(solution)/shard_map/psum | solution.py:20
  413.7 35.5 %all_to_all.12 = f32[8,1,1]{2,1,0:T(1,128)S(1)} all-to-all(f32[8,1,1]{2,1,0:T(1,128)S(1)} %broadcast_in_dim.43), channel_id=1, replica_groups=mesh['col_0'=4,'col_1'=4,'cuts'=8] {'cuts'}, dimensions={0} | all-to-all | bytes 64 | tf_op jit(solution)/shard_map/all_to_all | solution.py:26
  450.6 7.6 %all_to_all.13 = f32[8,1,2]{2,1,0:T(1,128)S(1)} all-to-all(f32[8,1,2]{2,1,0:T(1,128)S(1)} %broadcast_in_dim.44), channel_id=1, replica_groups=mesh['col_0'=4,'col_1'=4,'cuts'=8] {'cuts'}, dimensions={0} | all-to-all | bytes 128 | tf_op jit(solution)/shard_map/all_to_all | solution.py:26
  (287 shorter events, 180.2 us)
Async XLA Ops:
  16.0 11.5 %collective-permute-start = (f32[1,16,64,128]{3,2,1,0:T(8,128)S(1)}, f32[1,16,64,128]{3,2,1,0:T(8,128)S(1)}, u32[]{:S(2)}, u32[]{:S(2)}) collective-permute-start(f32[1,16,64,128]{3,2,1,0:T(8,128)S(1)} %get-tuple-element.477), channel_id=1, source_target_pairs={{0,8},{8,16},{16,24},{24,32},{32,40},{40,48},{48,56},{56,64},{64,7... | collective-permute-start | bytes 1572872 | tf_op jit(solution)/shard_map/while/body/eval_jaxpr/ppermute | solution.py:15
  17.3 10.1 %copy-start.3 = (f32[1,16,64,128]{3,2,1,0:T(8,128)S(1)}, f32[1,16,64,128]{3,2,1,0:T(8,128)}, u32[]{:S(2)}) copy-start(f32[1,16,64,128]{3,2,1,0:T(8,128)} %copy-done.2) | copy-start | bytes 1572868 | tf_op jit(solution)/shard_map/while
  37.2 13.4 %collective-permute-start = (f32[1,16,64,128]{3,2,1,0:T(8,128)S(1)}, f32[1,16,64,128]{3,2,1,0:T(8,128)S(1)}, u32[]{:S(2)}, u32[]{:S(2)}) collective-permute-start(f32[1,16,64,128]{3,2,1,0:T(8,128)S(1)} %get-tuple-element.477), channel_id=1, source_target_pairs={{0,8},{8,16},{16,24},{24,32},{32,40},{40,48},{48,56},{56,64},{64,7... | collective-permute-start | bytes 1572872 | tf_op jit(solution)/shard_map/while/body/eval_jaxpr/ppermute | solution.py:15
  60.4 12.6 %collective-permute-start = (f32[1,16,64,128]{3,2,1,0:T(8,128)S(1)}, f32[1,16,64,128]{3,2,1,0:T(8,128)S(1)}, u32[]{:S(2)}, u32[]{:S(2)}) collective-permute-start(f32[1,16,64,128]{3,2,1,0:T(8,128)S(1)} %get-tuple-element.477), channel_id=1, source_target_pairs={{0,8},{8,16},{16,24},{24,32},{32,40},{40,48},{48,56},{56,64},{64,7... | collective-permute-start | bytes 1572872 | tf_op jit(solution)/shard_map/while/body/eval_jaxpr/ppermute | solution.py:15
  82.7 11.7 %collective-permute-start = (f32[1,16,64,128]{3,2,1,0:T(8,128)S(1)}, f32[1,16,64,128]{3,2,1,0:T(8,128)S(1)}, u32[]{:S(2)}, u32[]{:S(2)}) collective-permute-start(f32[1,16,64,128]{3,2,1,0:T(8,128)S(1)} %get-tuple-element.477), channel_id=1, source_target_pairs={{0,8},{8,16},{16,24},{24,32},{32,40},{40,48},{48,56},{56,64},{64,7... | collective-permute-start | bytes 1572872 | tf_op jit(solution)/shard_map/while/body/eval_jaxpr/ppermute | solution.py:15
  95.2 19.8 %collective-permute-start = (f32[1,16,64,128]{3,2,1,0:T(8,128)S(1)}, f32[1,16,64,128]{3,2,1,0:T(8,128)S(1)}, u32[]{:S(2)}, u32[]{:S(2)}) collective-permute-start(f32[1,16,64,128]{3,2,1,0:T(8,128)S(1)} %get-tuple-element.477), channel_id=1, source_target_pairs={{0,8},{8,16},{16,24},{24,32},{32,40},{40,48},{48,56},{56,64},{64,7... | collective-permute-start | bytes 1572872 | tf_op jit(solution)/shard_map/while/body/eval_jaxpr/ppermute | solution.py:15
  115.8 10.2 %collective-permute-start = (f32[1,16,64,128]{3,2,1,0:T(8,128)S(1)}, f32[1,16,64,128]{3,2,1,0:T(8,128)S(1)}, u32[]{:S(2)}, u32[]{:S(2)}) collective-permute-start(f32[1,16,64,128]{3,2,1,0:T(8,128)S(1)} %get-tuple-element.477), channel_id=1, source_target_pairs={{0,8},{8,16},{16,24},{24,32},{32,40},{40,48},{48,56},{56,64},{64,7... | collective-permute-start | bytes 1572872 | tf_op jit(solution)/shard_map/while/body/eval_jaxpr/ppermute | solution.py:15
  126.8 18.1 %collective-permute-start = (f32[1,16,64,128]{3,2,1,0:T(8,128)S(1)}, f32[1,16,64,128]{3,2,1,0:T(8,128)S(1)}, u32[]{:S(2)}, u32[]{:S(2)}) collective-permute-start(f32[1,16,64,128]{3,2,1,0:T(8,128)S(1)} %get-tuple-element.477), channel_id=1, source_target_pairs={{0,8},{8,16},{16,24},{24,32},{32,40},{40,48},{48,56},{56,64},{64,7... | collective-permute-start | bytes 1572872 | tf_op jit(solution)/shard_map/while/body/eval_jaxpr/ppermute | solution.py:15
  145.8 11.4 %collective-permute-start = (f32[1,16,64,128]{3,2,1,0:T(8,128)S(1)}, f32[1,16,64,128]{3,2,1,0:T(8,128)S(1)}, u32[]{:S(2)}, u32[]{:S(2)}) collective-permute-start(f32[1,16,64,128]{3,2,1,0:T(8,128)S(1)} %get-tuple-element.477), channel_id=1, source_target_pairs={{0,8},{8,16},{16,24},{24,32},{32,40},{40,48},{48,56},{56,64},{64,7... | collective-permute-start | bytes 1572872 | tf_op jit(solution)/shard_map/while/body/eval_jaxpr/ppermute | solution.py:15
  158.0 19.8 %collective-permute-start = (f32[1,16,64,128]{3,2,1,0:T(8,128)S(1)}, f32[1,16,64,128]{3,2,1,0:T(8,128)S(1)}, u32[]{:S(2)}, u32[]{:S(2)}) collective-permute-start(f32[1,16,64,128]{3,2,1,0:T(8,128)S(1)} %get-tuple-element.477), channel_id=1, source_target_pairs={{0,8},{8,16},{16,24},{24,32},{32,40},{40,48},{48,56},{56,64},{64,7... | collective-permute-start | bytes 1572872 | tf_op jit(solution)/shard_map/while/body/eval_jaxpr/ppermute | solution.py:15
  178.6 12.4 %collective-permute-start = (f32[1,16,64,128]{3,2,1,0:T(8,128)S(1)}, f32[1,16,64,128]{3,2,1,0:T(8,128)S(1)}, u32[]{:S(2)}, u32[]{:S(2)}) collective-permute-start(f32[1,16,64,128]{3,2,1,0:T(8,128)S(1)} %get-tuple-element.477), channel_id=1, source_target_pairs={{0,8},{8,16},{16,24},{24,32},{32,40},{40,48},{48,56},{56,64},{64,7... | collective-permute-start | bytes 1572872 | tf_op jit(solution)/shard_map/while/body/eval_jaxpr/ppermute | solution.py:15
  191.8 20.9 %collective-permute-start = (f32[1,16,64,128]{3,2,1,0:T(8,128)S(1)}, f32[1,16,64,128]{3,2,1,0:T(8,128)S(1)}, u32[]{:S(2)}, u32[]{:S(2)}) collective-permute-start(f32[1,16,64,128]{3,2,1,0:T(8,128)S(1)} %get-tuple-element.477), channel_id=1, source_target_pairs={{0,8},{8,16},{16,24},{24,32},{32,40},{40,48},{48,56},{56,64},{64,7... | collective-permute-start | bytes 1572872 | tf_op jit(solution)/shard_map/while/body/eval_jaxpr/ppermute | solution.py:15
  213.5 16.5 %collective-permute-start = (f32[1,16,64,128]{3,2,1,0:T(8,128)S(1)}, f32[1,16,64,128]{3,2,1,0:T(8,128)S(1)}, u32[]{:S(2)}, u32[]{:S(2)}) collective-permute-start(f32[1,16,64,128]{3,2,1,0:T(8,128)S(1)} %get-tuple-element.477), channel_id=1, source_target_pairs={{0,8},{8,16},{16,24},{24,32},{32,40},{40,48},{48,56},{56,64},{64,7... | collective-permute-start | bytes 1572872 | tf_op jit(solution)/shard_map/while/body/eval_jaxpr/ppermute | solution.py:15
  230.9 13.4 %collective-permute-start = (f32[1,16,64,128]{3,2,1,0:T(8,128)S(1)}, f32[1,16,64,128]{3,2,1,0:T(8,128)S(1)}, u32[]{:S(2)}, u32[]{:S(2)}) collective-permute-start(f32[1,16,64,128]{3,2,1,0:T(8,128)S(1)} %get-tuple-element.477), channel_id=1, source_target_pairs={{0,8},{8,16},{16,24},{24,32},{32,40},{40,48},{48,56},{56,64},{64,7... | collective-permute-start | bytes 1572872 | tf_op jit(solution)/shard_map/while/body/eval_jaxpr/ppermute | solution.py:15
  245.1 28.1 %collective-permute-start = (f32[1,16,64,128]{3,2,1,0:T(8,128)S(1)}, f32[1,16,64,128]{3,2,1,0:T(8,128)S(1)}, u32[]{:S(2)}, u32[]{:S(2)}) collective-permute-start(f32[1,16,64,128]{3,2,1,0:T(8,128)S(1)} %get-tuple-element.477), channel_id=1, source_target_pairs={{0,8},{8,16},{16,24},{24,32},{32,40},{40,48},{48,56},{56,64},{64,7... | collective-permute-start | bytes 1572872 | tf_op jit(solution)/shard_map/while/body/eval_jaxpr/ppermute | solution.py:15
  262.1 11.1 %copy-start.3 = (f32[1,16,64,128]{3,2,1,0:T(8,128)S(1)}, f32[1,16,64,128]{3,2,1,0:T(8,128)}, u32[]{:S(2)}) copy-start(f32[1,16,64,128]{3,2,1,0:T(8,128)} %copy-done.2) | copy-start | bytes 1572868 | tf_op jit(solution)/shard_map/while
  274.0 16.1 %collective-permute-start = (f32[1,16,64,128]{3,2,1,0:T(8,128)S(1)}, f32[1,16,64,128]{3,2,1,0:T(8,128)S(1)}, u32[]{:S(2)}, u32[]{:S(2)}) collective-permute-start(f32[1,16,64,128]{3,2,1,0:T(8,128)S(1)} %get-tuple-element.477), channel_id=1, source_target_pairs={{0,8},{8,16},{16,24},{24,32},{32,40},{40,48},{48,56},{56,64},{64,7... | collective-permute-start | bytes 1572872 | tf_op jit(solution)/shard_map/while/body/eval_jaxpr/ppermute | solution.py:15
  280.2 10.0 %copy-start.3 = (f32[1,16,64,128]{3,2,1,0:T(8,128)S(1)}, f32[1,16,64,128]{3,2,1,0:T(8,128)}, u32[]{:S(2)}) copy-start(f32[1,16,64,128]{3,2,1,0:T(8,128)} %copy-done.2) | copy-start | bytes 1572868 | tf_op jit(solution)/shard_map/while
  291.0 13.9 %collective-permute-start = (f32[1,16,64,128]{3,2,1,0:T(8,128)S(1)}, f32[1,16,64,128]{3,2,1,0:T(8,128)S(1)}, u32[]{:S(2)}, u32[]{:S(2)}) collective-permute-start(f32[1,16,64,128]{3,2,1,0:T(8,128)S(1)} %get-tuple-element.477), channel_id=1, source_target_pairs={{0,8},{8,16},{16,24},{24,32},{32,40},{40,48},{48,56},{56,64},{64,7... | collective-permute-start | bytes 1572872 | tf_op jit(solution)/shard_map/while/body/eval_jaxpr/ppermute | solution.py:15
  305.7 14.2 %collective-permute-start = (f32[1,16,64,128]{3,2,1,0:T(8,128)S(1)}, f32[1,16,64,128]{3,2,1,0:T(8,128)S(1)}, u32[]{:S(2)}, u32[]{:S(2)}) collective-permute-start(f32[1,16,64,128]{3,2,1,0:T(8,128)S(1)} %get-tuple-element.477), channel_id=1, source_target_pairs={{0,8},{8,16},{16,24},{24,32},{32,40},{40,48},{48,56},{56,64},{64,7... | collective-permute-start | bytes 1572872 | tf_op jit(solution)/shard_map/while/body/eval_jaxpr/ppermute | solution.py:15
  320.7 13.3 %collective-permute-start = (f32[1,16,64,128]{3,2,1,0:T(8,128)S(1)}, f32[1,16,64,128]{3,2,1,0:T(8,128)S(1)}, u32[]{:S(2)}, u32[]{:S(2)}) collective-permute-start(f32[1,16,64,128]{3,2,1,0:T(8,128)S(1)} %get-tuple-element.477), channel_id=1, source_target_pairs={{0,8},{8,16},{16,24},{24,32},{32,40},{40,48},{48,56},{56,64},{64,7... | collective-permute-start | bytes 1572872 | tf_op jit(solution)/shard_map/while/body/eval_jaxpr/ppermute | solution.py:15
  334.9 12.3 %collective-permute-start = (f32[1,16,64,128]{3,2,1,0:T(8,128)S(1)}, f32[1,16,64,128]{3,2,1,0:T(8,128)S(1)}, u32[]{:S(2)}, u32[]{:S(2)}) collective-permute-start(f32[1,16,64,128]{3,2,1,0:T(8,128)S(1)} %get-tuple-element.477), channel_id=1, source_target_pairs={{0,8},{8,16},{16,24},{24,32},{32,40},{40,48},{48,56},{56,64},{64,7... | collective-permute-start | bytes 1572872 | tf_op jit(solution)/shard_map/while/body/eval_jaxpr/ppermute | solution.py:15
  412.5 37.4 %copy-start.10 = (f32[4]{0:T(128)}, f32[4]{0:T(128)S(1)}, u32[]{:S(2)}) copy-start(f32[4]{0:T(128)S(1)} %get-tuple-element.375) | copy-start | bytes 52
  412.5 38.0 %copy-start.8 = (f32[4,2]{0,1:T(2,128)}, f32[4,2]{0,1:T(2,128)S(1)}, u32[]{:S(2)}) copy-start(f32[4,2]{0,1:T(2,128)S(1)} %get-tuple-element.374) | copy-start | bytes 100
  (42 other events, 138.4 us)
where the time goes:
time: 460 us; the launch traced here: 459 us
  starting transfers between devices  141 us (31%)
  blocking collectives  108 us (23%)
  waiting for transfers between devices  100 us (22%)
  other arithmetic  31.4 us (7%)
  local copies, waits for them, and re-layouts  31.3 us (7%)
  loops' own time  28.7 us (6%)
  matrix products  16.6 us (4%)
    ppermute x19, starting transfers between devices, from_behind(): return lax.ppermute(value, axis, pairs)  141 us
    ppermute x19, waiting for transfers between devices, from_behind(): return lax.ppermute(value, axis, pairs)  100 us
    psum x2, blocking collectives, over_axes(): value = lax.psum(value, axis)  65.3 us
    all_to_all x2, blocking collectives, from_everyone(): lax.all_to_all(jnp.broadcast_to(value[None], (length, *value.shape)), axi...  43.1 us
    another operation x1, loops' own time, body(): lax.fori_loop(0, sections + groups - 1, section, initial)  23.5 us
    reduce_sum x19, other arithmetic, amplitude(): jnp.sum(b_real * c_real - b_imag * c_imag, axis=(1, 2, 3)) * factor  18.4 us
    while x76, local copies, waits for them, and re-layouts  14.3 us
  transfers between devices with their start and end apart: 19, of which 19 were waited for; matrix products, arithmetic and copies ran while one was open for 5% of the time, Pallas kernels for 0%

commit v1 on v0

--- a/solution.py
+++ b/solution.py
@@ -17,7 +17,7 @@
 
 def over_axes(value, axes):
     for axis in axes:
-        value = lax.psum(value, axis)
+        value = jnp.sum(lax.all_gather(value, axis), axis=0)
     return value
 
 

time: 460 us -> 476 us (1.035)
  starting transfers between devices: 141 us -> 172 us
  blocking collectives: 108 us -> 88.1 us
    psum x2 -> x0, blocking collectives: 65.3 us -> none  [over_axes(): value = lax.psum(value, axis)]
    unnamed x0 -> x2, blocking collectives: none -> 64.9 us
    all_to_all x0 -> x1, starting transfers between devices: none -> 31.2 us  [from_everyone(): lax.all_to_all(jnp.broadcast_to(value[None], (length, *value.shape)), axi...]
    all_to_all x2 -> x1, blocking collectives: 43.1 us -> 12.7 us  [from_everyone(): lax.all_to_all(jnp.broadcast_to(value[None], (length, *value.shape)), axi...]
    all_gather x0 -> x2, blocking collectives: none -> 10.5 us  [over_axes(): value = jnp.sum(lax.all_gather(value, axis), axis=0)]
  transfers between devices with their start and end apart: 19 -> 20, of which waited for: 19 -> 19; matrix products, arithmetic and copies ran while one was open for 5% -> 5% of each run, Pallas kernels for 0% -> 0%
where the time goes in v1:
time: 476 us; the launch traced here: 475 us
  starting transfers between devices  172 us (36%)
  waiting for transfers between devices  100 us (21%)
  blocking collectives  88.1 us (19%)
  local copies, waits for them, and re-layouts  34.8 us (7%)
  other arithmetic  31.5 us (7%)
  loops' own time  28.7 us (6%)
  matrix products  16.6 us (3%)
    ppermute x19, starting transfers between devices, from_behind(): return lax.ppermute(value, axis, pairs)  141 us
    ppermute x19, waiting for transfers between devices, from_behind(): return lax.ppermute(value, axis, pairs)  100 us
    unnamed x2, blocking collectives  64.9 us
    all_to_all x1, starting transfers between devices, from_everyone(): lax.all_to_all(jnp.broadcast_to(value[None], (length, *value.shape)), axi...  31.2 us
    another operation x1, loops' own time, body(): lax.fori_loop(0, sections + groups - 1, section, initial)  23.5 us
    reduce_sum x19, other arithmetic, amplitude(): jnp.sum(b_real * c_real - b_imag * c_imag, axis=(1, 2, 3)) * factor  18.4 us
    while x76, local copies, waits for them, and re-layouts  14.3 us
    all_to_all x1, blocking collectives, from_everyone(): lax.all_to_all(jnp.broadcast_to(value[None], (length, *value.shape)), axi...  12.7 us
  transfers between devices with their start and end apart: 20, of which 19 were waited for; matrix products, arithmetic and copies ran while one was open for 5% of the time, Pallas kernels for 0%

profile of v1, /device:TPU:1, one launch (start us, length us, event | category | flops | bytes accessed | tf_op | source)
XLA Modules:
  0.0 474.6 jit_solution(10498324926325785263)
XLA Ops:
  8.1 340.9 %while.18 = (s32[]{:T(128)}, f32[1,16,64,128]{3,2,1,0:T(8,128)S(1)}, f32[4,2]{0,1:T(2,128)S(1)}, f32[4]{0:T(128)S(1)}, s32[]{:T(128)}, /*index=5*/pred[]{:T(512)...) while((s32[]{:T(128)}, ...), condition=%wide.region_7.8_spmd, body=%wide.region_0.7_spmd.sunk | while | flops 404756480 | bytes 22449744 | solution.py:136
  8.9 8.9 %conditional.2 = (f32[1,16,64,128]{3,2,1,0:T(8,128)S(1)}, f32[1]{0:T(128)}) conditional(s32[]{:T(128)} %convert_element_type.12, f32[1,16,64,128]{3,2,1,0:T(8,128)S(1)} %broadcast_select_fusion.2, (f32[1,16,64,128]{3,2,1,0:T(8,128)S(1)}, f32[1,16,64,128]{3,2,1,0:T(8,128)}, f32[1,16,64,128]{3,2,1,0:T(8,128)S(1)}, s32[4,1]{0,1:T(1,128)S(1)}, s32[]{:T(128)}, ...), branch_computations={%region_1.1_spmd, %region_2.4_spmd} | conditional | flops 404101120 | bytes 13536336 | solution.py:114
  21.7 7.7 %collective-permute-done = f32[1,16,64,128]{3,2,1,0:T(8,128)S(1)} collective-permute-done((f32[1,16,64,128]{3,2,1,0:T(8,128)S(1)}, f32[1,16,64,128]{3,2,1,0:T(8,128)S(1)}, u32[]{:S(2)}, u32[]{:S(2)}) %collective-permute-start) | collective-permute-done | bytes 524320 | tf_op jit(solution)/shard_map/while/body/eval_jaxpr/ppermute | solution.py:15
  30.1 8.9 %conditional.2 = (f32[1,16,64,128]{3,2,1,0:T(8,128)S(1)}, f32[1]{0:T(128)}) conditional(s32[]{:T(128)} %convert_element_type.12, f32[1,16,64,128]{3,2,1,0:T(8,128)S(1)} %broadcast_select_fusion.2, (f32[1,16,64,128]{3,2,1,0:T(8,128)S(1)}, f32[1,16,64,128]{3,2,1,0:T(8,128)}, f32[1,16,64,128]{3,2,1,0:T(8,128)S(1)}, s32[4,1]{0,1:T(1,128)S(1)}, s32[]{:T(128)}, ...), branch_computations={%region_1.1_spmd, %region_2.4_spmd} | conditional | flops 404101120 | bytes 13536336 | solution.py:114
  45.7 6.7 %collective-permute-done = f32[1,16,64,128]{3,2,1,0:T(8,128)S(1)} collective-permute-done((f32[1,16,64,128]{3,2,1,0:T(8,128)S(1)}, f32[1,16,64,128]{3,2,1,0:T(8,128)S(1)}, u32[]{:S(2)}, u32[]{:S(2)}) %collective-permute-start) | collective-permute-done | bytes 524320 | tf_op jit(solution)/shard_map/while/body/eval_jaxpr/ppermute | solution.py:15
  53.3 8.9 %conditional.2 = (f32[1,16,64,128]{3,2,1,0:T(8,128)S(1)}, f32[1]{0:T(128)}) conditional(s32[]{:T(128)} %convert_element_type.12, f32[1,16,64,128]{3,2,1,0:T(8,128)S(1)} %broadcast_select_fusion.2, (f32[1,16,64,128]{3,2,1,0:T(8,128)S(1)}, f32[1,16,64,128]{3,2,1,0:T(8,128)}, f32[1,16,64,128]{3,2,1,0:T(8,128)S(1)}, s32[4,1]{0,1:T(1,128)S(1)}, s32[]{:T(128)}, ...), branch_computations={%region_1.1_spmd, %region_2.4_spmd} | conditional | flops 404101120 | bytes 13536336 | solution.py:114
  75.6 8.9 %conditional.2 = (f32[1,16,64,128]{3,2,1,0:T(8,128)S(1)}, f32[1]{0:T(128)}) conditional(s32[]{:T(128)} %convert_element_type.12, f32[1,16,64,128]{3,2,1,0:T(8,128)S(1)} %broadcast_select_fusion.2, (f32[1,16,64,128]{3,2,1,0:T(8,128)S(1)}, f32[1,16,64,128]{3,2,1,0:T(8,128)}, f32[1,16,64,128]{3,2,1,0:T(8,128)S(1)}, s32[4,1]{0,1:T(1,128)S(1)}, s32[]{:T(128)}, ...), branch_computations={%region_1.1_spmd, %region_2.4_spmd} | conditional | flops 404101120 | bytes 13536336 | solution.py:114
  97.1 13.1 %collective-permute-start = (f32[1,16,64,128]{3,2,1,0:T(8,128)S(1)}, f32[1,16,64,128]{3,2,1,0:T(8,128)S(1)}, u32[]{:S(2)}, u32[]{:S(2)}) collective-permute-start(f32[1,16,64,128]{3,2,1,0:T(8,128)S(1)} %get-tuple-element.487), channel_id=1, source_target_pairs={{0,8},{8,16},{16,24},{24,32},{32,40},{40,48},{48,56},{56,64},{64,7... | collective-permute-start | bytes 1572872 | tf_op jit(solution)/shard_map/while/body/eval_jaxpr/ppermute | solution.py:15
  128.7 12.0 %collective-permute-start = (f32[1,16,64,128]{3,2,1,0:T(8,128)S(1)}, f32[1,16,64,128]{3,2,1,0:T(8,128)S(1)}, u32[]{:S(2)}, u32[]{:S(2)}) collective-permute-start(f32[1,16,64,128]{3,2,1,0:T(8,128)S(1)} %get-tuple-element.487), channel_id=1, source_target_pairs={{0,8},{8,16},{16,24},{24,32},{32,40},{40,48},{48,56},{56,64},{64,7... | collective-permute-start | bytes 1572872 | tf_op jit(solution)/shard_map/while/body/eval_jaxpr/ppermute | solution.py:15
  159.8 13.7 %collective-permute-start = (f32[1,16,64,128]{3,2,1,0:T(8,128)S(1)}, f32[1,16,64,128]{3,2,1,0:T(8,128)S(1)}, u32[]{:S(2)}, u32[]{:S(2)}) collective-permute-start(f32[1,16,64,128]{3,2,1,0:T(8,128)S(1)} %get-tuple-element.487), channel_id=1, source_target_pairs={{0,8},{8,16},{16,24},{24,32},{32,40},{40,48},{48,56},{56,64},{64,7... | collective-permute-start | bytes 1572872 | tf_op jit(solution)/shard_map/while/body/eval_jaxpr/ppermute | solution.py:15
  180.4 6.2 %collective-permute-start = (f32[1,16,64,128]{3,2,1,0:T(8,128)S(1)}, f32[1,16,64,128]{3,2,1,0:T(8,128)S(1)}, u32[]{:S(2)}, u32[]{:S(2)}) collective-permute-start(f32[1,16,64,128]{3,2,1,0:T(8,128)S(1)} %get-tuple-element.487), channel_id=1, source_target_pairs={{0,8},{8,16},{16,24},{24,32},{32,40},{40,48},{48,56},{56,64},{64,7... | collective-permute-start | bytes 1572872 | tf_op jit(solution)/shard_map/while/body/eval_jaxpr/ppermute | solution.py:15
  193.6 14.8 %collective-permute-start = (f32[1,16,64,128]{3,2,1,0:T(8,128)S(1)}, f32[1,16,64,128]{3,2,1,0:T(8,128)S(1)}, u32[]{:S(2)}, u32[]{:S(2)}) collective-permute-start(f32[1,16,64,128]{3,2,1,0:T(8,128)S(1)} %get-tuple-element.487), channel_id=1, source_target_pairs={{0,8},{8,16},{16,24},{24,32},{32,40},{40,48},{48,56},{56,64},{64,7... | collective-permute-start | bytes 1572872 | tf_op jit(solution)/shard_map/while/body/eval_jaxpr/ppermute | solution.py:15
  215.3 8.1 %collective-permute-start = (f32[1,16,64,128]{3,2,1,0:T(8,128)S(1)}, f32[1,16,64,128]{3,2,1,0:T(8,128)S(1)}, u32[]{:S(2)}, u32[]{:S(2)}) collective-permute-start(f32[1,16,64,128]{3,2,1,0:T(8,128)S(1)} %get-tuple-element.487), channel_id=1, source_target_pairs={{0,8},{8,16},{16,24},{24,32},{32,40},{40,48},{48,56},{56,64},{64,7... | collective-permute-start | bytes 1572872 | tf_op jit(solution)/shard_map/while/body/eval_jaxpr/ppermute | solution.py:15
  239.4 6.6 %collective-permute-done = f32[1,16,64,128]{3,2,1,0:T(8,128)S(1)} collective-permute-done((f32[1,16,64,128]{3,2,1,0:T(8,128)S(1)}, f32[1,16,64,128]{3,2,1,0:T(8,128)S(1)}, u32[]{:S(2)}, u32[]{:S(2)}) %collective-permute-start) | collective-permute-done | bytes 524320 | tf_op jit(solution)/shard_map/while/body/eval_jaxpr/ppermute | solution.py:15
  246.9 17.0 %collective-permute-start = (f32[1,16,64,128]{3,2,1,0:T(8,128)S(1)}, f32[1,16,64,128]{3,2,1,0:T(8,128)S(1)}, u32[]{:S(2)}, u32[]{:S(2)}) collective-permute-start(f32[1,16,64,128]{3,2,1,0:T(8,128)S(1)} %get-tuple-element.487), channel_id=1, source_target_pairs={{0,8},{8,16},{16,24},{24,32},{32,40},{40,48},{48,56},{56,64},{64,7... | collective-permute-start | bytes 1572872 | tf_op jit(solution)/shard_map/while/body/eval_jaxpr/ppermute | solution.py:15
  266.4 8.6 %collective-permute-done = f32[1,16,64,128]{3,2,1,0:T(8,128)S(1)} collective-permute-done((f32[1,16,64,128]{3,2,1,0:T(8,128)S(1)}, f32[1,16,64,128]{3,2,1,0:T(8,128)S(1)}, u32[]{:S(2)}, u32[]{:S(2)}) %collective-permute-start) | collective-permute-done | bytes 524320 | tf_op jit(solution)/shard_map/while/body/eval_jaxpr/ppermute | solution.py:15
  284.5 7.4 %collective-permute-done = f32[1,16,64,128]{3,2,1,0:T(8,128)S(1)} collective-permute-done((f32[1,16,64,128]{3,2,1,0:T(8,128)S(1)}, f32[1,16,64,128]{3,2,1,0:T(8,128)S(1)}, u32[]{:S(2)}, u32[]{:S(2)}) %collective-permute-start) | collective-permute-done | bytes 524320 | tf_op jit(solution)/shard_map/while/body/eval_jaxpr/ppermute | solution.py:15
  300.4 6.3 %collective-permute-done = f32[1,16,64,128]{3,2,1,0:T(8,128)S(1)} collective-permute-done((f32[1,16,64,128]{3,2,1,0:T(8,128)S(1)}, f32[1,16,64,128]{3,2,1,0:T(8,128)S(1)}, u32[]{:S(2)}, u32[]{:S(2)}) %collective-permute-start) | collective-permute-done | bytes 524320 | tf_op jit(solution)/shard_map/while/body/eval_jaxpr/ppermute | solution.py:15
  307.5 6.2 %collective-permute-start = (f32[1,16,64,128]{3,2,1,0:T(8,128)S(1)}, f32[1,16,64,128]{3,2,1,0:T(8,128)S(1)}, u32[]{:S(2)}, u32[]{:S(2)}) collective-permute-start(f32[1,16,64,128]{3,2,1,0:T(8,128)S(1)} %get-tuple-element.487), channel_id=1, source_target_pairs={{0,8},{8,16},{16,24},{24,32},{32,40},{40,48},{48,56},{56,64},{64,7... | collective-permute-start | bytes 1572872 | tf_op jit(solution)/shard_map/while/body/eval_jaxpr/ppermute | solution.py:15
  322.5 6.2 %collective-permute-start = (f32[1,16,64,128]{3,2,1,0:T(8,128)S(1)}, f32[1,16,64,128]{3,2,1,0:T(8,128)S(1)}, u32[]{:S(2)}, u32[]{:S(2)}) collective-permute-start(f32[1,16,64,128]{3,2,1,0:T(8,128)S(1)} %get-tuple-element.487), channel_id=1, source_target_pairs={{0,8},{8,16},{16,24},{24,32},{32,40},{40,48},{48,56},{56,64},{64,7... | collective-permute-start | bytes 1572872 | tf_op jit(solution)/shard_map/while/body/eval_jaxpr/ppermute | solution.py:15
  349.2 54.1 %all-reduce.1 = f32[16]{0:T(128)S(1)} all-reduce(f32[16]{0:T(128)S(1)} %dynamic-update-slice.8), channel_id=4, replica_groups=mesh['col_0'=4,'col_1'=4,'cuts'=8] {'col_0'}, use_global_device_ids=true, to_apply=%add.1 | all-reduce | flops 16 | bytes 128
  405.5 10.8 %all-reduce.2 = f32[16]{0:T(128)S(1)} all-reduce(f32[16]{0:T(128)S(1)} %dynamic-update-slice.9), channel_id=5, replica_groups=mesh['col_0'=4,'col_1'=4,'cuts'=8] {'col_1'}, use_global_device_ids=true, to_apply=%add.2 | all-reduce | flops 16 | bytes 128
  418.3 31.2 %all-to-all-start = ((f32[8,1,1]{2,1,0:T(1,128)}), f32[8,1,1]{2,1,0:T(1,128)S(1)}, u32[]{:S(2)}, u32[]{:S(2)}) async-start(f32[8,1,1]{2,1,0:T(1,128)} %broadcast_in_dim.43), calls=%async_computation | async-start | bytes 8192 | tf_op jit(solution)/shard_map/all_to_all | solution.py:26
  461.4 12.7 %all_to_all.12 = f32[8,1,2]{2,1,0:T(1,128)S(1)} all-to-all(f32[8,1,2]{2,1,0:T(1,128)S(1)} %broadcast_in_dim.44), channel_id=1, replica_groups=mesh['col_0'=4,'col_1'=4,'cuts'=8] {'cuts'}, dimensions={0} | all-to-all | bytes 128 | tf_op jit(solution)/shard_map/all_to_all | solution.py:26
  (306 shorter events, 194.3 us)
Async XLA Ops:
  17.9 11.5 %collective-permute-start = (f32[1,16,64,128]{3,2,1,0:T(8,128)S(1)}, f32[1,16,64,128]{3,2,1,0:T(8,128)S(1)}, u32[]{:S(2)}, u32[]{:S(2)}) collective-permute-start(f32[1,16,64,128]{3,2,1,0:T(8,128)S(1)} %get-tuple-element.487), channel_id=1, source_target_pairs={{0,8},{8,16},{16,24},{24,32},{32,40},{40,48},{48,56},{56,64},{64,7... | collective-permute-start | bytes 1572872 | tf_op jit(solution)/shard_map/while/body/eval_jaxpr/ppermute | solution.py:15
  19.2 10.1 %copy-start.3 = (f32[1,16,64,128]{3,2,1,0:T(8,128)S(1)}, f32[1,16,64,128]{3,2,1,0:T(8,128)}, u32[]{:S(2)}) copy-start(f32[1,16,64,128]{3,2,1,0:T(8,128)} %copy-done.2) | copy-start | bytes 1572868 | tf_op jit(solution)/shard_map/while
  39.1 13.4 %collective-permute-start = (f32[1,16,64,128]{3,2,1,0:T(8,128)S(1)}, f32[1,16,64,128]{3,2,1,0:T(8,128)S(1)}, u32[]{:S(2)}, u32[]{:S(2)}) collective-permute-start(f32[1,16,64,128]{3,2,1,0:T(8,128)S(1)} %get-tuple-element.487), channel_id=1, source_target_pairs={{0,8},{8,16},{16,24},{24,32},{32,40},{40,48},{48,56},{56,64},{64,7... | collective-permute-start | bytes 1572872 | tf_op jit(solution)/shard_map/while/body/eval_jaxpr/ppermute | solution.py:15
  62.2 12.6 %collective-permute-start = (f32[1,16,64,128]{3,2,1,0:T(8,128)S(1)}, f32[1,16,64,128]{3,2,1,0:T(8,128)S(1)}, u32[]{:S(2)}, u32[]{:S(2)}) collective-permute-start(f32[1,16,64,128]{3,2,1,0:T(8,128)S(1)} %get-tuple-element.487), channel_id=1, source_target_pairs={{0,8},{8,16},{16,24},{24,32},{32,40},{40,48},{48,56},{56,64},{64,7... | collective-permute-start | bytes 1572872 | tf_op jit(solution)/shard_map/while/body/eval_jaxpr/ppermute | solution.py:15
  84.5 11.7 %collective-permute-start = (f32[1,16,64,128]{3,2,1,0:T(8,128)S(1)}, f32[1,16,64,128]{3,2,1,0:T(8,128)S(1)}, u32[]{:S(2)}, u32[]{:S(2)}) collective-permute-start(f32[1,16,64,128]{3,2,1,0:T(8,128)S(1)} %get-tuple-element.487), channel_id=1, source_target_pairs={{0,8},{8,16},{16,24},{24,32},{32,40},{40,48},{48,56},{56,64},{64,7... | collective-permute-start | bytes 1572872 | tf_op jit(solution)/shard_map/while/body/eval_jaxpr/ppermute | solution.py:15
  97.1 19.8 %collective-permute-start = (f32[1,16,64,128]{3,2,1,0:T(8,128)S(1)}, f32[1,16,64,128]{3,2,1,0:T(8,128)S(1)}, u32[]{:S(2)}, u32[]{:S(2)}) collective-permute-start(f32[1,16,64,128]{3,2,1,0:T(8,128)S(1)} %get-tuple-element.487), channel_id=1, source_target_pairs={{0,8},{8,16},{16,24},{24,32},{32,40},{40,48},{48,56},{56,64},{64,7... | collective-permute-start | bytes 1572872 | tf_op jit(solution)/shard_map/while/body/eval_jaxpr/ppermute | solution.py:15
  117.6 10.2 %collective-permute-start = (f32[1,16,64,128]{3,2,1,0:T(8,128)S(1)}, f32[1,16,64,128]{3,2,1,0:T(8,128)S(1)}, u32[]{:S(2)}, u32[]{:S(2)}) collective-permute-start(f32[1,16,64,128]{3,2,1,0:T(8,128)S(1)} %get-tuple-element.487), channel_id=1, source_target_pairs={{0,8},{8,16},{16,24},{24,32},{32,40},{40,48},{48,56},{56,64},{64,7... | collective-permute-start | bytes 1572872 | tf_op jit(solution)/shard_map/while/body/eval_jaxpr/ppermute | solution.py:15
  128.7 18.1 %collective-permute-start = (f32[1,16,64,128]{3,2,1,0:T(8,128)S(1)}, f32[1,16,64,128]{3,2,1,0:T(8,128)S(1)}, u32[]{:S(2)}, u32[]{:S(2)}) collective-permute-start(f32[1,16,64,128]{3,2,1,0:T(8,128)S(1)} %get-tuple-element.487), channel_id=1, source_target_pairs={{0,8},{8,16},{16,24},{24,32},{32,40},{40,48},{48,56},{56,64},{64,7... | collective-permute-start | bytes 1572872 | tf_op jit(solution)/shard_map/while/body/eval_jaxpr/ppermute | solution.py:15
  147.6 11.4 %collective-permute-start = (f32[1,16,64,128]{3,2,1,0:T(8,128)S(1)}, f32[1,16,64,128]{3,2,1,0:T(8,128)S(1)}, u32[]{:S(2)}, u32[]{:S(2)}) collective-permute-start(f32[1,16,64,128]{3,2,1,0:T(8,128)S(1)} %get-tuple-element.487), channel_id=1, source_target_pairs={{0,8},{8,16},{16,24},{24,32},{32,40},{40,48},{48,56},{56,64},{64,7... | collective-permute-start | bytes 1572872 | tf_op jit(solution)/shard_map/while/body/eval_jaxpr/ppermute | solution.py:15
  159.8 19.8 %collective-permute-start = (f32[1,16,64,128]{3,2,1,0:T(8,128)S(1)}, f32[1,16,64,128]{3,2,1,0:T(8,128)S(1)}, u32[]{:S(2)}, u32[]{:S(2)}) collective-permute-start(f32[1,16,64,128]{3,2,1,0:T(8,128)S(1)} %get-tuple-element.487), channel_id=1, source_target_pairs={{0,8},{8,16},{16,24},{24,32},{32,40},{40,48},{48,56},{56,64},{64,7... | collective-permute-start | bytes 1572872 | tf_op jit(solution)/shard_map/while/body/eval_jaxpr/ppermute | solution.py:15
  180.4 12.4 %collective-permute-start = (f32[1,16,64,128]{3,2,1,0:T(8,128)S(1)}, f32[1,16,64,128]{3,2,1,0:T(8,128)S(1)}, u32[]{:S(2)}, u32[]{:S(2)}) collective-permute-start(f32[1,16,64,128]{3,2,1,0:T(8,128)S(1)} %get-tuple-element.487), channel_id=1, source_target_pairs={{0,8},{8,16},{16,24},{24,32},{32,40},{40,48},{48,56},{56,64},{64,7... | collective-permute-start | bytes 1572872 | tf_op jit(solution)/shard_map/while/body/eval_jaxpr/ppermute | solution.py:15
  193.6 20.9 %collective-permute-start = (f32[1,16,64,128]{3,2,1,0:T(8,128)S(1)}, f32[1,16,64,128]{3,2,1,0:T(8,128)S(1)}, u32[]{:S(2)}, u32[]{:S(2)}) collective-permute-start(f32[1,16,64,128]{3,2,1,0:T(8,128)S(1)} %get-tuple-element.487), channel_id=1, source_target_pairs={{0,8},{8,16},{16,24},{24,32},{32,40},{40,48},{48,56},{56,64},{64,7... | collective-permute-start | bytes 1572872 | tf_op jit(solution)/shard_map/while/body/eval_jaxpr/ppermute | solution.py:15
  215.3 16.5 %collective-permute-start = (f32[1,16,64,128]{3,2,1,0:T(8,128)S(1)}, f32[1,16,64,128]{3,2,1,0:T(8,128)S(1)}, u32[]{:S(2)}, u32[]{:S(2)}) collective-permute-start(f32[1,16,64,128]{3,2,1,0:T(8,128)S(1)} %get-tuple-element.487), channel_id=1, source_target_pairs={{0,8},{8,16},{16,24},{24,32},{32,40},{40,48},{48,56},{56,64},{64,7... | collective-permute-start | bytes 1572872 | tf_op jit(solution)/shard_map/while/body/eval_jaxpr/ppermute | solution.py:15
  232.7 13.4 %collective-permute-start = (f32[1,16,64,128]{3,2,1,0:T(8,128)S(1)}, f32[1,16,64,128]{3,2,1,0:T(8,128)S(1)}, u32[]{:S(2)}, u32[]{:S(2)}) collective-permute-start(f32[1,16,64,128]{3,2,1,0:T(8,128)S(1)} %get-tuple-element.487), channel_id=1, source_target_pairs={{0,8},{8,16},{16,24},{24,32},{32,40},{40,48},{48,56},{56,64},{64,7... | collective-permute-start | bytes 1572872 | tf_op jit(solution)/shard_map/while/body/eval_jaxpr/ppermute | solution.py:15
  246.9 28.1 %collective-permute-start = (f32[1,16,64,128]{3,2,1,0:T(8,128)S(1)}, f32[1,16,64,128]{3,2,1,0:T(8,128)S(1)}, u32[]{:S(2)}, u32[]{:S(2)}) collective-permute-start(f32[1,16,64,128]{3,2,1,0:T(8,128)S(1)} %get-tuple-element.487), channel_id=1, source_target_pairs={{0,8},{8,16},{16,24},{24,32},{32,40},{40,48},{48,56},{56,64},{64,7... | collective-permute-start | bytes 1572872 | tf_op jit(solution)/shard_map/while/body/eval_jaxpr/ppermute | solution.py:15
  263.9 11.1 %copy-start.3 = (f32[1,16,64,128]{3,2,1,0:T(8,128)S(1)}, f32[1,16,64,128]{3,2,1,0:T(8,128)}, u32[]{:S(2)}) copy-start(f32[1,16,64,128]{3,2,1,0:T(8,128)} %copy-done.2) | copy-start | bytes 1572868 | tf_op jit(solution)/shard_map/while
  275.8 16.2 %collective-permute-start = (f32[1,16,64,128]{3,2,1,0:T(8,128)S(1)}, f32[1,16,64,128]{3,2,1,0:T(8,128)S(1)}, u32[]{:S(2)}, u32[]{:S(2)}) collective-permute-start(f32[1,16,64,128]{3,2,1,0:T(8,128)S(1)} %get-tuple-element.487), channel_id=1, source_target_pairs={{0,8},{8,16},{16,24},{24,32},{32,40},{40,48},{48,56},{56,64},{64,7... | collective-permute-start | bytes 1572872 | tf_op jit(solution)/shard_map/while/body/eval_jaxpr/ppermute | solution.py:15
  282.0 10.0 %copy-start.3 = (f32[1,16,64,128]{3,2,1,0:T(8,128)S(1)}, f32[1,16,64,128]{3,2,1,0:T(8,128)}, u32[]{:S(2)}) copy-start(f32[1,16,64,128]{3,2,1,0:T(8,128)} %copy-done.2) | copy-start | bytes 1572868 | tf_op jit(solution)/shard_map/while
  292.8 13.9 %collective-permute-start = (f32[1,16,64,128]{3,2,1,0:T(8,128)S(1)}, f32[1,16,64,128]{3,2,1,0:T(8,128)S(1)}, u32[]{:S(2)}, u32[]{:S(2)}) collective-permute-start(f32[1,16,64,128]{3,2,1,0:T(8,128)S(1)} %get-tuple-element.487), channel_id=1, source_target_pairs={{0,8},{8,16},{16,24},{24,32},{32,40},{40,48},{48,56},{56,64},{64,7... | collective-permute-start | bytes 1572872 | tf_op jit(solution)/shard_map/while/body/eval_jaxpr/ppermute | solution.py:15
  307.5 14.2 %collective-permute-start = (f32[1,16,64,128]{3,2,1,0:T(8,128)S(1)}, f32[1,16,64,128]{3,2,1,0:T(8,128)S(1)}, u32[]{:S(2)}, u32[]{:S(2)}) collective-permute-start(f32[1,16,64,128]{3,2,1,0:T(8,128)S(1)} %get-tuple-element.487), channel_id=1, source_target_pairs={{0,8},{8,16},{16,24},{24,32},{32,40},{40,48},{48,56},{56,64},{64,7... | collective-permute-start | bytes 1572872 | tf_op jit(solution)/shard_map/while/body/eval_jaxpr/ppermute | solution.py:15
  322.5 13.3 %collective-permute-start = (f32[1,16,64,128]{3,2,1,0:T(8,128)S(1)}, f32[1,16,64,128]{3,2,1,0:T(8,128)S(1)}, u32[]{:S(2)}, u32[]{:S(2)}) collective-permute-start(f32[1,16,64,128]{3,2,1,0:T(8,128)S(1)} %get-tuple-element.487), channel_id=1, source_target_pairs={{0,8},{8,16},{16,24},{24,32},{32,40},{40,48},{48,56},{56,64},{64,7... | collective-permute-start | bytes 1572872 | tf_op jit(solution)/shard_map/while/body/eval_jaxpr/ppermute | solution.py:15
  336.7 12.3 %collective-permute-start = (f32[1,16,64,128]{3,2,1,0:T(8,128)S(1)}, f32[1,16,64,128]{3,2,1,0:T(8,128)S(1)}, u32[]{:S(2)}, u32[]{:S(2)}) collective-permute-start(f32[1,16,64,128]{3,2,1,0:T(8,128)S(1)} %get-tuple-element.487), channel_id=1, source_target_pairs={{0,8},{8,16},{16,24},{24,32},{32,40},{40,48},{48,56},{56,64},{64,7... | collective-permute-start | bytes 1572872 | tf_op jit(solution)/shard_map/while/body/eval_jaxpr/ppermute | solution.py:15
  416.4 44.2 %copy-start.9 = (f32[4]{0:T(128)}, f32[4]{0:T(128)S(1)}, u32[]{:S(2)}) copy-start(f32[4]{0:T(128)S(1)} %reduce_sum.79) | copy-start | bytes 52
  418.3 41.7 %all-to-all-start = ((f32[8,1,1]{2,1,0:T(1,128)}), f32[8,1,1]{2,1,0:T(1,128)S(1)}, u32[]{:S(2)}, u32[]{:S(2)}) async-start(f32[8,1,1]{2,1,0:T(1,128)} %broadcast_in_dim.43), calls=%async_computation | async-start | bytes 8192 | tf_op jit(solution)/shard_map/all_to_all | solution.py:26
  (45 other events, 142.6 us)
